TPU v7x, 32 devices: a whole 2x2x4 slice. The times are simulated.
32 devices in a mesh: seq: 4 (over z), wt: 8 (over y, x, core).
Axes of the slice: x: 2, y: 2, z: 4, core: 2. Of those that a mesh axis runs over, the one named last changes fastest.
Arguments:
- tokens: bfloat16 [8, 512, 2048], P('wt', 'seq'), may hold values from -6 to 6
- cotangent: bfloat16 [8, 512, 2048], P('wt', 'seq'), may hold values from -6 to 6
- segment_ids: int32 [8, 512], P('wt'), may hold values from 0 to 1, never falling along the last dimension, each value on 1 to 320 neighbouring positions
- expert_routes: int32 [8, 512, 8], P('wt', 'seq'), may hold values from 0 to 15, all different within a row; in each aligned block of 128 rows (0 to 127, 128 to 255, ..., all dimensions but the last counted through in order) at most 128 rows name the same one
- w_qkv: bfloat16 [2048, 6144], P('wt'), may hold values from -0.125 to 0.125
- w_out: bfloat16 [2048, 2048], P('wt'), may hold values from -2 to 2
- w_router: bfloat16 [2048, 16], P('wt'), may hold values from -0.0625 to 0.0625
- w_gate_up: bfloat16 [16, 2048, 2048], P('seq', 'wt'), may hold values from -0.125 to 0.125
- w_down: bfloat16 [16, 1024, 2048], P('seq', 'wt'), may hold values from -0.75 to 0.75
- attn_gain: bfloat16 [2048], P('wt'), may hold values from 0.5 to 1.5
- ffn_gain: bfloat16 [2048], P('wt'), may hold values from 0.5 to 1.5
- q_gain: bfloat16 [128], P('wt'), may hold values from 0.5 to 1.5
- k_gain: bfloat16 [128], P('wt'), may hold values from 0.5 to 1.5
Outputs:
- output: bfloat16 [8, 512, 2048], P('wt', 'seq')
- tokens_grad: float32 [8, 512, 2048], P('wt', 'seq')
- w_qkv_grad: float32 [2048, 6144], P('wt')
- w_out_grad: float32 [2048, 2048], P('wt')
- w_router_grad: float32 [2048, 16], P('wt')
- w_gate_up_grad: float32 [16, 2048, 2048], P('seq', 'wt')
- w_down_grad: float32 [16, 1024, 2048], P('seq', 'wt')
- attn_gain_grad: float32 [2048], P('wt')
- ffn_gain_grad: float32 [2048], P('wt')
- q_gain_grad: float32 [128], P('wt')
- k_gain_grad: float32 [128], P('wt')
Inputs may be any that keep to these rules, and one draw needn't show every extreme that they name: `segment_ids`: along a sequence the segment numbers never fall; each of the 2 documents spans 1 to 320 positions. `expert_routes`: A token names 8 different experts; among the 128 tokens of one device no expert is named more than 128 times, a bound that some block reaches.
All inputs are finite; a program needn't handle non-finite values.
Results may differ from a plain program's by a relative error of at most 0.028.
Values may be sent and summed in bfloat16 or wider, within the bound.
A program may use at most 512 MiB of HBM per device.

v0:
```python
import jax
import jax.numpy as jnp
import numpy as np
from jax import lax
from jax.sharding import PartitionSpec as P

H = 16
HD = 128
FF = 1024
EPS = 1e-06
THETA = 50000.0
NEG = -1e30
LANES = 128
BF = jnp.bfloat16
F32 = jnp.float32


def normalize(values):
    factor = lax.rsqrt(jnp.mean(values * values, axis=-1, keepdims=True) + EPS)
    return (values * factor, factor)


def norm_back(grad_normed, normed_values, factor):
    return factor * (
        grad_normed - normed_values * jnp.mean(grad_normed * normed_values, axis=-1, keepdims=True)
    )


def rope_tables(length):
    half = HD // 2
    freq = THETA ** (-jnp.arange(half, dtype=F32) * 2.0 / HD)
    angle = jnp.arange(length, dtype=F32)[:, None] * freq[None, :]
    return (jnp.cos(angle)[:, None, :], jnp.sin(angle)[:, None, :])


def rotate(values, cosine, sine):
    half = values.shape[-1] // 2
    first = values[..., :half]
    second = values[..., half:]
    return jnp.concatenate(
        [first * cosine - second * sine, second * cosine + first * sine], axis=-1
    )


def dot(left, right, dims):
    return lax.dot_general(left, right, (dims, ((), ())), preferred_element_type=F32)


def nn(left, right):
    return dot(left, right, ((1,), (0,)))


def nt(left, right):
    return dot(left, right, ((1,), (1,)))


def tn(left, right):
    return dot(left, right, ((0,), (0,)))


def split_two(values):
    high = values.astype(BF)
    low = (values - high.astype(F32)).astype(BF)
    return (high, low)


def body(
    tokens,
    cotangent,
    segment_ids,
    expert_routes,
    w_qkv,
    w_out,
    w_router,
    w_gate_up,
    w_down,
    attn_gain,
    ffn_gain,
    q_gain,
    k_gain,
):
    seq_total = lax.axis_size("seq")
    wt_total = lax.axis_size("wt")
    seq_me = lax.axis_index("seq")
    rows = tokens.shape[1]
    model = tokens.shape[2]
    length = rows * seq_total
    shard = w_qkv.shape[0]
    local_experts = w_gate_up.shape[0]
    experts = w_router.shape[1]
    heads = H // seq_total
    cols = 3 * heads * HD
    gain_part = q_gain.shape[0]
    tokens_all = lax.all_gather(tokens[0], "seq", axis=0, tiled=True)
    routes_all = lax.all_gather(expert_routes[0], "seq", axis=0, tiled=True)
    w_here = lax.dynamic_slice_in_dim(
        w_qkv.reshape(shard, 3, seq_total, heads * HD), seq_me, 1, axis=2
    ).reshape(shard, cols)
    small = jnp.concatenate(
        [
            w_router,
            attn_gain[:, None],
            ffn_gain[:, None],
            jnp.pad(q_gain, (0, shard - gain_part))[:, None],
            jnp.pad(k_gain, (0, shard - gain_part))[:, None],
        ],
        axis=1,
    )
    small = jnp.pad(small, ((0, 0), (0, LANES - small.shape[1])))
    qkv_full = lax.all_gather(jnp.concatenate([w_here, small], axis=1), "wt", axis=0, tiled=True)
    out_full = lax.all_gather(w_out, "wt", axis=0, tiled=True)
    grad_all = lax.all_gather(cotangent[0], "seq", axis=0, tiled=True)
    expert_full = [
        lax.all_gather(jnp.concatenate([w_gate_up[e], w_down[e]], axis=0), "wt", axis=0)
        for e in range(local_experts)
    ]
    small_full = qkv_full[:, cols:]
    router_full = small_full[:, :experts]
    picker = np.zeros((8, LANES), np.float32)
    for row in range(4):
        picker[row, experts + row] = 1.0
    gain_rows = nt(jnp.asarray(picker, BF), small_full)
    gain_attn = gain_rows[0]
    gain_ffn = gain_rows[1]
    gain_query = gain_rows[2].reshape(wt_total, shard)[:, :gain_part].reshape(HD)
    gain_key = gain_rows[3].reshape(wt_total, shard)[:, :gain_part].reshape(HD)
    segments = segment_ids[0]
    same = segments[:, None] == segments[None, :]
    cosine, sine = rope_tables(length)
    normed_all, _ = normalize(tokens_all.astype(F32))
    hidden = (normed_all * gain_attn).astype(BF)
    projected = nn(hidden, qkv_full)[:, :cols].reshape(length, 3, heads, HD)
    normed_q, factor_q = normalize(projected[:, 0])
    normed_k, factor_k = normalize(projected[:, 1])
    queries = jnp.swapaxes(rotate(normed_q * gain_query, cosine, sine).astype(BF), 0, 1)
    keys = jnp.swapaxes(rotate(normed_k * gain_key, cosine, sine).astype(BF), 0, 1)
    values = jnp.swapaxes(projected[:, 2].astype(BF), 0, 1)
    scale = HD ** (-0.5)

    def bmm(left, right, dims):
        return lax.dot_general(left, right, (dims, ((0,), (0,))), preferred_element_type=F32)

    logits = jnp.where(same[None], bmm(queries, keys, ((2,), (2,))) * scale, NEG)
    powers = jnp.exp(logits - jnp.max(logits, axis=-1, keepdims=True))
    weights = powers / jnp.sum(powers, axis=-1, keepdims=True)
    weights_low = weights.astype(BF)
    attended = bmm(weights_low, values, ((2,), (1,))).astype(BF)
    merged = lax.all_to_all(
        jnp.swapaxes(attended, 0, 1), "seq", split_axis=0, concat_axis=1, tiled=True
    ).reshape(rows, H * HD)
    inputs = tokens[0].astype(F32)
    residual = inputs + nn(merged, out_full)
    normed_f, factor_f = normalize(residual)
    hidden_own = (normed_f * gain_ffn).astype(BF)
    hidden_ffn = lax.all_gather(hidden_own, "seq", axis=0, tiled=True)
    chances = jax.nn.softmax(nn(hidden_ffn, router_full), axis=-1)
    expert_ids = jnp.arange(experts, dtype=jnp.int32)
    routed = jnp.any(routes_all[:, :, None] == expert_ids[None, None, :], axis=1)
    picked = jnp.where(routed, chances, 0.0)
    picked_total = jnp.sum(picked, axis=1, keepdims=True)
    gates = picked / picked_total
    gates_here = lax.dynamic_slice_in_dim(gates, seq_me * local_experts, local_experts, axis=1)
    out_part = jnp.zeros((length, model), F32)
    grad_hidden_part = jnp.zeros((length, model), F32)
    gate_grads = []
    expert_grads = []
    for e in range(local_experts):
        gate = gates_here[:, e : e + 1]
        gate_up = expert_full[e][:, : model // wt_total].reshape(model, 2 * FF)
        down = expert_full[e][:, model // wt_total :].reshape(FF, model)
        before = nn(hidden_ffn, gate_up)
        gate_part = before[:, :FF]
        up_part = before[:, FF:]
        sigmoid_gate = jax.nn.sigmoid(gate_part)
        silu_gate = gate_part * sigmoid_gate
        activated = silu_gate * up_part
        scaled = (gate * activated).astype(BF)
        grad_act = nt(grad_all, down)
        gate_grads.append(jnp.sum(grad_act * activated, axis=1, keepdims=True))
        grad_act = grad_act * gate
        grad_gate = grad_act * up_part * sigmoid_gate * (1.0 + gate_part * (1.0 - sigmoid_gate))
        grad_up = grad_act * silu_gate
        grad_before = jnp.concatenate([grad_gate, grad_up], axis=-1).astype(BF)
        out_part = out_part + nn(scaled, down)
        grad_hidden_part = grad_hidden_part + nt(grad_before, gate_up)
        gate_up_grad = tn(hidden_ffn, grad_before).astype(BF)
        down_grad = tn(scaled, grad_all).astype(BF)
        joined = jnp.concatenate(
            [
                gate_up_grad.reshape(wt_total, model // wt_total, 2 * FF),
                down_grad.reshape(wt_total, FF // wt_total, model),
            ],
            axis=1,
        )
        expert_grads.append(
            lax.psum_scatter(joined, "wt", scatter_dimension=0, tiled=False).astype(F32)
        )
    gate_up_out = jnp.stack([g[: model // wt_total] for g in expert_grads])
    down_out = jnp.stack([g[model // wt_total :] for g in expert_grads])
    gate_grad_part = jnp.concatenate(gate_grads, axis=1)
    gate_high, gate_low = split_two(gate_grad_part)

    def spread(part):
        wide = jnp.zeros((length, experts), BF)
        return lax.dynamic_update_slice(wide, part, (0, seq_me * local_experts))

    returned = lax.psum_scatter(
        jnp.concatenate([grad_hidden_part.astype(BF), spread(gate_high), spread(gate_low)], axis=1),
        "seq",
        scatter_dimension=0,
        tiled=True,
    ).astype(F32)
    grad_hidden = returned[:, :model]
    gate_grad = returned[:, model : model + experts] + returned[:, model + experts :]
    moe_out = lax.psum_scatter(out_part.astype(BF), "seq", scatter_dimension=0, tiled=True).astype(
        F32
    )
    output = (residual + moe_out).astype(BF)

    def own(full):
        return lax.dynamic_slice_in_dim(full, seq_me * rows, rows, axis=0)

    chances_own = own(chances)
    routed_own = own(routed)
    gates_own = own(gates)
    inner_gate = jnp.sum(gate_grad * gates_own, axis=1, keepdims=True)
    grad_chances = jnp.where(routed_own, (gate_grad - inner_gate) / own(picked_total), 0.0)
    grad_logits = (
        chances_own * (grad_chances - jnp.sum(grad_chances * chances_own, axis=1, keepdims=True))
    ).astype(BF)
    grad_hidden = grad_hidden + nt(grad_logits, router_full)
    router_grad = tn(hidden_own, grad_logits)
    ffn_gain_grad = jnp.sum(grad_hidden * normed_f, axis=0)
    grad_residual = cotangent[0].astype(F32) + norm_back(grad_hidden * gain_ffn, normed_f, factor_f)
    grad_branch = grad_residual.astype(BF)
    grad_merged = nt(grad_branch, out_full).astype(BF).reshape(rows, H, HD)
    grad_heads = jnp.swapaxes(
        lax.all_to_all(grad_merged, "seq", split_axis=1, concat_axis=0, tiled=True), 0, 1
    )
    out_grad = lax.psum_scatter(
        tn(merged, grad_branch).astype(BF), "wt", scatter_dimension=0, tiled=True
    )
    out_grad = lax.psum(out_grad, "seq").astype(F32)
    grad_weights = bmm(grad_heads, values, ((2,), (2,)))
    inner = jnp.sum(weights * grad_weights, axis=-1, keepdims=True)
    grad_scores = (weights * (grad_weights - inner)).astype(BF)
    grad_q = jnp.swapaxes(bmm(grad_scores, keys, ((2,), (1,))), 0, 1) * scale
    grad_k = jnp.swapaxes(bmm(grad_scores, queries, ((1,), (1,))), 0, 1) * scale
    grad_v = jnp.swapaxes(bmm(weights_low, grad_heads, ((1,), (1,))), 0, 1)
    grad_q_normed = rotate(grad_q, cosine, -sine)
    grad_k_normed = rotate(grad_k, cosine, -sine)
    q_gain_grad = jnp.sum(grad_q_normed * normed_q, axis=(0, 1))
    k_gain_grad = jnp.sum(grad_k_normed * normed_k, axis=(0, 1))
    grad_q_raw = norm_back(grad_q_normed * gain_query, normed_q, factor_q)
    grad_k_raw = norm_back(grad_k_normed * gain_key, normed_k, factor_k)
    grad_projected = (
        jnp.stack([grad_q_raw, grad_k_raw, grad_v], axis=1).reshape(length, cols).astype(BF)
    )
    qkv_grad = tn(hidden, grad_projected)
    grad_normed_part = nt(jnp.pad(grad_projected, ((0, 0), (0, LANES))), qkv_full)
    attn_gain_grad = jnp.sum(grad_normed_part * normed_all, axis=0)
    grad_normed_own = lax.psum_scatter(
        grad_normed_part.astype(BF), "seq", scatter_dimension=0, tiled=True
    ).astype(F32)
    normed_a, factor_a = normalize(inputs)
    tokens_grad = grad_residual + norm_back(grad_normed_own * gain_attn, normed_a, factor_a)

    def gain_column(vector):
        return jnp.pad(
            vector.reshape(wt_total, gain_part), ((0, 0), (0, shard - gain_part))
        ).reshape(model, 1)

    small_grad = jnp.concatenate(
        [
            router_grad,
            attn_gain_grad[:, None],
            ffn_gain_grad[:, None],
            gain_column(q_gain_grad),
            gain_column(k_gain_grad),
        ],
        axis=1,
    )
    small_grad = jnp.pad(small_grad, ((0, 0), (0, LANES - small_grad.shape[1])))
    scattered = lax.psum_scatter(
        jnp.concatenate([qkv_grad, small_grad], axis=1).astype(BF),
        "wt",
        scatter_dimension=0,
        tiled=True,
    )
    collected = lax.all_gather(scattered, "seq", axis=0).astype(F32)
    qkv_out = (
        collected[:, :, :cols]
        .reshape(seq_total, shard, 3, heads * HD)
        .transpose(1, 2, 0, 3)
        .reshape(shard, 3 * H * HD)
    )
    small_out = jnp.sum(collected[:, :, cols:], axis=0)
    return (
        output[None],
        tokens_grad[None],
        qkv_out,
        out_grad,
        small_out[:, :experts],
        gate_up_out,
        down_out,
        small_out[:, experts],
        small_out[:, experts + 1],
        small_out[:gain_part, experts + 2],
        small_out[:gain_part, experts + 3],
    )


def solution(mesh):
    in_specs = (
        P("wt", "seq", None),
        P("wt", "seq", None),
        P("wt", None),
        P("wt", "seq", None),
        P("wt", None),
        P("wt", None),
        P("wt", None),
        P("seq", "wt", None),
        P("seq", "wt", None),
        P("wt"),
        P("wt"),
        P("wt"),
        P("wt"),
    )
    out_specs = (
        P("wt", "seq", None),
        P("wt", "seq", None),
        P("wt", None),
        P("wt", None),
        P("wt", None),
        P("seq", "wt", None),
        P("seq", "wt", None),
        P("wt"),
        P("wt"),
        P("wt"),
        P("wt"),
    )
    return jax.shard_map(body, mesh=mesh, in_specs=in_specs, out_specs=out_specs, check_vma=False)
```

profile of v0, /device:TPU:0, one launch (start us, length us, event | category | flops | bytes accessed | tf_op | source)
XLA Modules:
  0.0 1457.3 jit_solution(14407658807051301885)
XLA Ops:
  18.4 39.6 %all-gather.25.cloned.1.call-done = bf16[1,512,2048]{2,1,0:T(8,128)(2,1)} async-done(((bf16[1,128,2048]{2,1,0:T(8,128)(2,1)}), bf16[1,512,2048]{2,1,0:T(8,128)(2,1)}) %all-gather.25.cloned.1.call-update) | async-done | bytes 2097168 | tf_op jit(solution)/shard_map/all_gather | solution.py:94
  60.1 48.1 %all-gather.19.cloned.1.call-done = bf16[2048,1664]{0,1:T(8,128)(2,1)} async-done(((bf16[256,1664]{0,1:T(8,128)(2,1)}), bf16[2048,1664]{0,1:T(8,128)(2,1)}) %all-gather.19.cloned.1.call-update) | async-done | bytes 6815760 | tf_op jit(solution)/shard_map/all_gather | solution.py:110
  110.0 8.6 fusion.3
  133.7 19.4 %all_to_all.33 = bf16[512,4,128]{2,1,0:T(4,128)(2,1)S(1)} all-to-all(bf16[512,4,128]{2,1,0:T(4,128)(2,1)S(1)} %copy.163), channel_id=1, replica_groups=mesh['seq'=4,'wt'=8] {'seq'}, dimensions={0} | all-to-all | bytes 1048576 | tf_op jit(solution)/shard_map/all_to_all | solution.py:148
  153.4 10.9 all-gather.21.cloned.1.call-done
  164.4 4.9 multiply_reduce_fusion.7
  182.9 13.9 all-gather.1
  197.0 20.3 %all-gather.23.cloned.1.call-done = bf16[512,2048]{1,0:T(8,128)(2,1)} async-done(((bf16[128,2048]{1,0:T(8,128)(2,1)}), bf16[512,2048]{1,0:T(8,128)(2,1)}) %all-gather.23.cloned.1.call-update) | async-done | bytes 2097168 | tf_op jit(solution)/shard_map/all_gather | solution.py:155
  222.4 68.0 %all-gather.31.cloned.1.call-done = bf16[3072,2048]{1,0:T(8,128)(2,1)} async-done(((bf16[384,2048]{1,0:T(8,128)(2,1)}), bf16[3072,2048]{1,0:T(8,128)(2,1)}) %all-gather.31.cloned.1.call-update) | async-done | bytes 12582928 | tf_op jit(solution)/shard_map/all_gather | solution.py:114
  290.4 8.4 slice.299
  298.9 5.4 slice.302
  304.3 60.5 %all-gather.27.cloned.1.call-done = bf16[3072,2048]{1,0:T(8,128)(2,1)} async-done(((bf16[384,2048]{1,0:T(8,128)(2,1)}), bf16[3072,2048]{1,0:T(8,128)(2,1)}) %all-gather.27.cloned.1.call-update) | async-done | bytes 12582928 | tf_op jit(solution)/shard_map/all_gather | solution.py:114
  364.8 8.3 slice.291
  373.1 5.4 slice.294
  378.5 60.2 %all-gather.29.cloned.1.call-done = bf16[3072,2048]{1,0:T(8,128)(2,1)} async-done(((bf16[384,2048]{1,0:T(8,128)(2,1)}), bf16[3072,2048]{1,0:T(8,128)(2,1)}) %all-gather.29.cloned.1.call-update) | async-done | bytes 12582928 | tf_op jit(solution)/shard_map/all_gather | solution.py:114
  438.7 8.3 slice.295
  447.0 5.5 slice.298
  452.5 60.1 %all-gather.33.cloned.1.call-done = bf16[3072,2048]{1,0:T(8,128)(2,1)} async-done(((bf16[384,2048]{1,0:T(8,128)(2,1)}), bf16[3072,2048]{1,0:T(8,128)(2,1)}) %all-gather.33.cloned.1.call-update) | async-done | bytes 12582928 | tf_op jit(solution)/shard_map/all_gather | solution.py:114
  512.6 8.3 slice.303
  520.9 5.2 slice.306
  526.1 9.6 fusion.110
  535.7 6.1 fusion.106
  541.8 6.1 fusion.108
  547.9 6.5 fusion.112
  554.5 5.4 all-gather.35.cloned.1.call-done
  559.9 9.1 multiply_convert_fusion.4
  569.0 4.6 multiply_convert_fusion.8
  573.6 4.9 multiply_convert_fusion.6
  578.6 4.6 multiply_convert_fusion.2
  583.8 10.7 fusion.39
  594.5 9.7 fusion.41
  604.3 6.2 fusion.40
  611.5 12.3 add_convert_fusion
  626.8 5.0 fusion.111
  642.1 30.1 %reduce-scatter.12.cloned.1.call-done = bf16[128,2080]{1,0:T(8,128)(2,1)} async-done(((bf16[512,2080]{1,0:T(8,128)(2,1)}), bf16[128,2080]{1,0:T(8,128)(2,1)}) %reduce-scatter.12.cloned.1.call-update) | async-done | bytes 532496 | tf_op jit(solution)/shard_map/reduce_scatter | solution.py:207
  677.6 40.4 %reduce-scatter.10.cloned.1.call-done = bf16[128,2048]{1,0:T(8,128)(2,1)} async-done(((bf16[512,2048]{1,0:T(8,128)(2,1)}), bf16[128,2048]{1,0:T(8,128)(2,1)}) %reduce-scatter.10.cloned.1.call-update) | async-done | bytes 524304 | tf_op jit(solution)/shard_map/reduce_scatter | solution.py:215
  720.5 5.7 convolution_convert_fusion.5
  726.3 6.3 fusion.46
  737.4 14.1 all-to-all-done.1
  768.3 9.8 fusion.8
  778.4 5.6 convolution_convert_fusion
  784.0 7.9 fusion.2
  792.5 4.6 reduce-scatter.18.cloned.1.call-done
  797.4 6.9 convolution_convert_fusion.1
  806.8 9.1 pad_maximum_fusion.3
  817.1 4.1 convolution_convert_fusion.7
  821.3 5.0 convolution_convert_fusion.2
  826.3 9.1 pad_maximum_fusion.2
  836.6 4.2 convolution_convert_fusion.8
  840.9 5.0 convolution_convert_fusion.3
  845.9 9.1 pad_maximum_fusion.1
  860.3 5.0 convolution_convert_fusion.4
  865.3 9.0 pad_maximum_fusion
  875.6 35.4 %reduce-scatter.14.cloned.1.call-done = bf16[128,2048]{1,0:T(8,128)(2,1)} async-done(((bf16[512,2048]{1,0:T(8,128)(2,1)}), bf16[128,2048]{1,0:T(8,128)(2,1)}) %reduce-scatter.14.cloned.1.call-update) | async-done | bytes 524304 | tf_op jit(solution)/shard_map/reduce_scatter | solution.py:262
  914.8 49.5 %all-reduce.9.cloned.1.call-done = bf16[256,2048]{1,0:T(8,128)(2,1)} async-done(((bf16[256,2048]{1,0:T(8,128)(2,1)}), bf16[256,2048]{1,0:T(8,128)(2,1)}) %all-reduce.9.cloned.1.call-update) | async-done | bytes 1048592 | tf_op jit(solution)/shard_map/psum | solution.py:243
  967.1 92.2 %reduce-scatter.26.cloned.1.call-done = bf16[1,384,2048]{2,1,0:T(8,128)(2,1)} async-done(((bf16[8,384,2048]{2,1,0:T(8,128)(2,1)}), bf16[1,384,2048]{2,1,0:T(8,128)(2,1)}) %reduce-scatter.26.cloned.1.call-update) | async-done | bytes 1572880 | tf_op jit(solution)/shard_map/reduce_scatter | solution.py:196
  1061.1 93.8 %reduce-scatter.24.cloned.1.call-done = bf16[1,384,2048]{2,1,0:T(8,128)(2,1)} async-done(((bf16[8,384,2048]{2,1,0:T(8,128)(2,1)}), bf16[1,384,2048]{2,1,0:T(8,128)(2,1)}) %reduce-scatter.24.cloned.1.call-update) | async-done | bytes 1572880 | tf_op jit(solution)/shard_map/reduce_scatter | solution.py:196
  1158.9 91.7 %reduce-scatter.22.cloned.1.call-done = bf16[1,384,2048]{2,1,0:T(8,128)(2,1)} async-done(((bf16[8,384,2048]{2,1,0:T(8,128)(2,1)}), bf16[1,384,2048]{2,1,0:T(8,128)(2,1)}) %reduce-scatter.22.cloned.1.call-update) | async-done | bytes 1572880 | tf_op jit(solution)/shard_map/reduce_scatter | solution.py:196
  1254.6 91.8 %reduce-scatter.20.cloned.1.call-done = bf16[1,384,2048]{2,1,0:T(8,128)(2,1)} async-done(((bf16[8,384,2048]{2,1,0:T(8,128)(2,1)}), bf16[1,384,2048]{2,1,0:T(8,128)(2,1)}) %reduce-scatter.20.cloned.1.call-update) | async-done | bytes 1572880 | tf_op jit(solution)/shard_map/reduce_scatter | solution.py:196
  1356.2 59.4 %all-gather.37.cloned.1.call-done = bf16[1024,1664]{0,1:T(8,128)(2,1)} async-done(((bf16[256,1664]{0,1:T(8,128)(2,1)}), bf16[1024,1664]{0,1:T(8,128)(2,1)}) %all-gather.37.cloned.1.call-update) | async-done | bytes 3407888 | tf_op jit(solution)/shard_map/all_gather | solution.py:290
  1415.6 7.9 reshape.383
  1423.5 6.8 slice.314
  1433.3 8.7 copy.187
  1442.0 8.3 reshape.363
  (379 shorter events, 134.8 us)
Async XLA Ops:
  7.2 6.7 copy-start.69
  7.2 50.8 %all-gather.25.cloned.1.call-start = ((), (), s32[]{:S(2)}) async-start(), calls=%async_computation.24 | async-start | bytes 2621440 | tf_op jit(solution)/shard_map/all_gather | solution.py:94
  7.9 100.2 %all-gather.19.cloned.1.call-start = ((), (), s32[]{:S(2)}) async-start(), calls=%async_computation.11 | async-start | bytes 7667712 | tf_op jit(solution)/shard_map/all_gather | solution.py:110
  10.6 5.1 copy-start.63
  13.8 94.4 %copy-start.73 = (bf16[8,128]{1,0:T(8,128)(2,1)S(1)}, bf16[8,128]{1,0:T(8,128)(2,1)}, u32[]{:S(2)}) copy-start(bf16[8,128]{1,0:T(8,128)(2,1)} %constant.61.clone) | copy-start | bytes 6148
  14.9 149.4 %all-gather.21.cloned.1.call-start = ((), (), s32[]{:S(2)}) async-start(), calls=%async_computation.12 | async-start | bytes 9437184 | tf_op jit(solution)/shard_map/all_gather | solution.py:111
  15.7 201.6 %all-gather.23.cloned.1.call-start = ((), (), s32[]{:S(2)}) async-start(), calls=%async_computation.13 | async-start | bytes 2621440 | tf_op jit(solution)/shard_map/all_gather | solution.py:155
  18.4 106.9 %copy-start.28 = (f32[512,64]{1,0:T(8,128)}, f32[512,64]{1,0:T(8,128)S(1)}, u32[]{:S(2)}) copy-start(f32[512,64]{1,0:T(8,128)S(1)} %get-tuple-element.77) | copy-start | bytes 393220
  60.1 49.4 %copy-start.74 = (f32[512]{0:T(512)}, f32[512]{0:T(512)S(1)}, u32[]{:S(2)}) copy-start(f32[512]{0:T(512)S(1)} %add_rsqrt_fusion.2) | copy-start | bytes 6148
  109.5 59.8 %copy-start.53 = (f32[1,2048]{1,0:T(1,128)}, f32[1,2048]{1,0:T(1,128)S(1)}, u32[]{:S(2)}) copy-start(f32[1,2048]{1,0:T(1,128)S(1)} %get-tuple-element.73) | copy-start | bytes 24580
  133.3 31.1 %copy-start.6 = (bf16[1,128,2048]{2,1,0:T(8,128)(2,1)S(1)}, bf16[1,128,2048]{2,1,0:T(8,128)(2,1)}, u32[]{:S(2)}) copy-start(bf16[1,128,2048]{2,1,0:T(8,128)(2,1)} %param.14) | copy-start | bytes 1572868
  153.4 15.8 %copy-start.8 = (bf16[128,4,4,128]{0,3,2,1:T(8,128)(2,1)}, bf16[128,4,4,128]{0,3,2,1:T(8,128)(2,1)S(1)}, u32[]{:S(2)}) copy-start(bf16[128,4,4,128]{0,3,2,1:T(8,128)(2,1)S(1)} %copy.165) | copy-start | bytes 1572868
  164.3 6.9 copy-start.34
  169.3 5.2 copy-start.70
  171.2 119.2 %all-gather.31.cloned.1.call-start = ((), (), s32[]{:S(2)}) async-start(), calls=%async_computation.27 | async-start | bytes 14155776 | tf_op jit(solution)/shard_map/all_gather | solution.py:114
  175.8 189.0 %all-gather.27.cloned.1.call-start = ((), (), s32[]{:S(2)}) async-start(), calls=%async_computation.25 | async-start | bytes 14155776 | tf_op jit(solution)/shard_map/all_gather | solution.py:114
  178.2 260.5 %all-gather.29.cloned.1.call-start = ((), (), s32[]{:S(2)}) async-start(), calls=%async_computation.26 | async-start | bytes 14155776 | tf_op jit(solution)/shard_map/all_gather | solution.py:114
  180.8 331.8 %all-gather.33.cloned.1.call-start = ((), (), s32[]{:S(2)}) async-start(), calls=%async_computation.28 | async-start | bytes 14155776 | tf_op jit(solution)/shard_map/all_gather | solution.py:114
  182.1 377.8 %all-gather.35.cloned.1.call-start = ((), (), s32[]{:S(2)}) async-start(), calls=%async_computation.29 | async-start | bytes 2621440 | tf_op jit(solution)/shard_map/all_gather | solution.py:112
  182.8 489.3 %reduce-scatter.12.cloned.1.call-start = ((), (), s32[]{:S(2)}) async-start(), calls=%async_computation.15 | async-start | bytes 2785280 | tf_op jit(solution)/shard_map/reduce_scatter | solution.py:207
  197.0 101.9 %copy-start.49 = (pred[512,16]{1,0:T(8,128)(4,1)}, pred[512,16]{1,0:T(8,128)(4,1)S(1)}, u32[]{:S(2)}) copy-start(pred[512,16]{1,0:T(8,128)(4,1)S(1)} %copy.167) | copy-start | bytes 24580
  220.2 78.6 %copy-start.64 = (f32[512]{0:T(512)}, f32[512]{0:T(512)S(1)}, u32[]{:S(2)}) copy-start(f32[512]{0:T(512)S(1)} %get-tuple-element.25) | copy-start | bytes 6148
  520.9 5.2 copy-start.30
  520.9 14.8 %slice-start = ((s8[8388608]{0:T(1024)(128)(4,1)}), s8[4194304]{0:T(1024)(128)(4,1)S(1)}, s32[]{:S(2)}) async-start(s8[8388608]{0:T(1024)(128)(4,1)} %bitcast.299), calls=%async_computation.31 | async-start | bytes 8388608
  526.1 9.6 slice-start.1
  526.1 15.8 %slice-start.4 = ((s8[8388608]{0:T(1024)(128)(4,1)}), s8[4194304]{0:T(1024)(128)(4,1)S(1)}, s32[]{:S(2)}) async-start(s8[8388608]{0:T(1024)(128)(4,1)} %bitcast.306), calls=%async_computation.35 | async-start | bytes 8388608
  535.7 6.1 slice-start.5
  535.7 12.3 slice-start.2
  541.8 6.1 slice-start.3
  559.9 9.1 copy-start.20
  559.9 9.1 copy-start.76
  559.9 9.1 copy-start.87
  573.6 20.9 %copy-start.88 = (bf16[512,1024]{1,0:T(8,128)(2,1)}, bf16[512,1024]{1,0:T(8,128)(2,1)S(1)}, u32[]{:S(2)}) copy-start(bf16[512,1024]{1,0:T(8,128)(2,1)S(1)} %get-tuple-element.31) | copy-start | bytes 3145732
  583.2 53.8 %copy-start.78 = (bf16[512,1024]{1,0:T(8,128)(2,1)}, bf16[512,1024]{1,0:T(8,128)(2,1)S(1)}, u32[]{:S(2)}) copy-start(bf16[512,1024]{1,0:T(8,128)(2,1)S(1)} %get-tuple-element.39) | copy-start | bytes 3145732
  583.8 10.7 copy-start.90
  583.8 20.5 %slice-start.6 = ((s8[8388608]{0:T(1024)(128)(4,1)}), s8[4194304]{0:T(1024)(128)(4,1)S(1)}, s32[]{:S(2)}) async-start(s8[8388608]{0:T(1024)(128)(4,1)} %bitcast.309), calls=%async_computation.37 | async-start | bytes 8388608
  594.5 9.7 slice-start.7
  594.5 9.7 copy-start.92
  594.5 9.7 copy-start.94
  626.7 91.3 %reduce-scatter.10.cloned.1.call-start = ((), (), s32[]{:S(2)}) async-start(), calls=%async_computation.14 | async-start | bytes 2621440 | tf_op jit(solution)/shard_map/reduce_scatter | solution.py:215
  626.8 5.0 copy-start.21
  626.8 5.0 copy-start.80
  637.0 37.4 %copy-start.46 = (f32[512,16]{1,0:T(8,128)S(1)}, f32[512,16]{1,0:T(8,128)}, u32[]{:S(2)}) copy-start(f32[512,16]{1,0:T(8,128)} %copy-done.45) | copy-start | bytes 98308
  640.8 34.6 %copy-start.5 = (f32[128,2048]{1,0:T(8,128)S(1)}, f32[128,2048]{1,0:T(8,128)}, u32[]{:S(2)}) copy-start(f32[128,2048]{1,0:T(8,128)} %copy-done.4) | copy-start | bytes 3145732
  640.8 34.6 %copy-start.54 = (f32[1,2048]{1,0:T(1,128)S(1)}, f32[1,2048]{1,0:T(1,128)}, u32[]{:S(2)}) copy-start(f32[1,2048]{1,0:T(1,128)} %copy-done.53) | copy-start | bytes 24580
  640.8 34.6 %copy-start.71 = (f32[128]{0:T(128)S(1)}, f32[128]{0:T(128)}, u32[]{:S(2)}) copy-start(f32[128]{0:T(128)} %copy-done.70) | copy-start | bytes 1540
  640.8 77.2 %copy-start.35 = (bf16[1,128,2048]{2,1,0:T(8,128)(2,1)S(1)}, bf16[1,128,2048]{2,1,0:T(8,128)(2,1)}, u32[]{:S(2)}) copy-start(bf16[1,128,2048]{2,1,0:T(8,128)(2,1)} %param.15) | copy-start | bytes 1572868
  640.9 156.3 %reduce-scatter.18.cloned.1.call-start = ((), (), s32[]{:S(2)}) async-start(), calls=%async_computation.18 | async-start | bytes 9437184 | tf_op jit(solution)/shard_map/reduce_scatter | solution.py:240
  674.3 46.2 %copy-start.9 = (bf16[128,4,4,128]{0,3,2,1:T(8,128)(2,1)S(1)}, bf16[128,4,4,128]{0,3,2,1:T(8,128)(2,1)}, u32[]{:S(2)}) copy-start(bf16[128,4,4,128]{0,3,2,1:T(8,128)(2,1)} %copy-done.8) | copy-start | bytes 1572868
  726.3 10.9 copy-start.17
  726.3 25.2 %copy-start.51 = (bf16[512,1,4,128]{3,2,1,0:T(4,128)(2,1)S(1)}, bf16[512,1,4,128]{3,2,1,0:T(4,128)(2,1)}, u32[]{:S(2)}) copy-start(bf16[512,1,4,128]{3,2,1,0:T(4,128)(2,1)} %slice.288) | copy-start | bytes 1572868
  726.3 25.2 %copy-start.62 = (f32[4,512]{1,0:T(4,128)S(1)}, f32[4,512]{1,0:T(4,128)}, u32[]{:S(2)}) copy-start(f32[4,512]{1,0:T(4,128)} %copy-done.61) | copy-start | bytes 24580
  733.6 17.9 %all-to-all-start.1 = ((bf16[128,16,128]{2,0,1:T(8,128)(2,1)}), bf16[128,16,128]{2,0,1:T(8,128)(2,1)S(1)}, u32[]{:S(2)}, u32[]{:S(2)}) async-start(bf16[128,16,128]{2,0,1:T(8,128)(2,1)} %bitcast.275), calls=%async_computation.3 | async-start | bytes 1048576 | tf_op jit(solution)/shard_map/all_to_all | solution.py:238
  737.1 137.4 %reduce-scatter.16.cloned.1.call-start = ((), (), s32[]{:S(2)}) async-start(), calls=%async_computation.17 | async-start | bytes 7667712 | tf_op jit(solution)/shard_map/reduce_scatter | solution.py:284
  768.3 10.1 copy-start.60
  791.9 119.1 %reduce-scatter.14.cloned.1.call-start = ((), (), s32[]{:S(2)}) async-start(), calls=%async_computation.16 | async-start | bytes 2621440 | tf_op jit(solution)/shard_map/reduce_scatter | solution.py:262
  792.5 171.9 %all-reduce.9.cloned.1.call-start = ((), (), s32[]{:S(2)}) async-start(), calls=%async_computation.19 | async-start | bytes 2097152 | tf_op jit(solution)/shard_map/psum | solution.py:243
  797.1 7.2 copy-start.79
  797.2 262.1 %reduce-scatter.26.cloned.1.call-start = ((), (), s32[]{:S(2)}) async-start(), calls=%async_computation.23 | async-start | bytes 14155776 | tf_op jit(solution)/shard_map/reduce_scatter | solution.py:196
  797.4 6.9 copy-start.77
  815.9 339.1 %reduce-scatter.24.cloned.1.call-start = ((), (), s32[]{:S(2)}) async-start(), calls=%async_computation.22 | async-start | bytes 14155776 | tf_op jit(solution)/shard_map/reduce_scatter | solution.py:196
  835.4 415.2 %reduce-scatter.22.cloned.1.call-start = ((), (), s32[]{:S(2)}) async-start(), calls=%async_computation.21 | async-start | bytes 14155776 | tf_op jit(solution)/shard_map/reduce_scatter | solution.py:196
  855.0 491.5 %reduce-scatter.20.cloned.1.call-start = ((), (), s32[]{:S(2)}) async-start(), calls=%async_computation.20 | async-start | bytes 14155776 | tf_op jit(solution)/shard_map/reduce_scatter | solution.py:196
  874.4 541.2 %all-gather.37.cloned.1.call-start = ((), (), s32[]{:S(2)}) async-start(), calls=%async_computation.30 | async-start | bytes 4259840 | tf_op jit(solution)/shard_map/all_gather | solution.py:290
  (63 other events, 161.4 us)
Sparse Core Ops, SparseCore 0:
  9.6 48.3 all-gather.24
  60.4 47.6 all-gather.18
  110.1 54.2 all-gather.20
  171.3 45.9 all-gather.22
  219.6 70.7 all-gather.30
  292.7 71.9 all-gather.26
  366.7 71.9 all-gather.28
  440.6 71.9 all-gather.32
  514.2 45.6 all-gather.34
  626.8 45.2 reduce-scatter.11
  675.0 42.9 reduce-scatter.9
  726.4 70.6 reduce-scatter.17
  800.6 64.0 reduce-scatter.15
  867.4 43.6 reduce-scatter.13
  913.2 51.0 all-reduce.8
  967.7 91.5 reduce-scatter.25
  1062.6 92.2 reduce-scatter.23
  1158.3 92.2 reduce-scatter.21
  1254.1 92.2 reduce-scatter.19
  1347.9 67.6 all-gather.36
where the time goes:
time: 1470 us; the launch traced here: 1460 us
  waiting for transfers between devices  979 us (67%)
  matrix products  200 us (14%)
  local copies, waits for them, and re-layouts  134 us (9%)
  other arithmetic  88.7 us (6%)
  blocking collectives  33.2 us (2%)
  between operations  16 us (1%)
    reduce_scatter x4, waiting for transfers between devices, body(): lax.psum_scatter(joined, 'wt', scatter_dimension=0, tiled=False).astype(F32)  369 us
    all_gather x4, waiting for transfers between devices, body(): lax.all_gather(jnp.concatenate([w_gate_up[e], w_down[e]], axis=0), 'wt',...  249 us
    dot_general x34, matrix products, dot(): lax.dot_general(left, right, (dims, ((), ())), preferred_element_type=F32)  188 us
    all_gather x1, waiting for transfers between devices, body(): collected = lax.all_gather(scattered, 'seq', axis=0).astype(F32)  59.4 us
    psum x1, waiting for transfers between devices, body(): out_grad = lax.psum(out_grad, 'seq').astype(F32)  49.5 us
    all_gather x1, waiting for transfers between devices, body(): lax.all_gather(jnp.concatenate([w_here, small], axis=1), 'wt', axis=0, ti...  48.1 us
    reduce_scatter x1, waiting for transfers between devices, body(): lax.psum_scatter(out_part.astype(BF), 'seq', scatter_dimension=0, tiled=T...  40.4 us
    all_gather x1, waiting for transfers between devices, body(): tokens_all = lax.all_gather(tokens[0], 'seq', axis=0, tiled=True)  39.6 us
  transfers between devices with their start and end apart: 21, of which 20 were waited for; matrix products, arithmetic and copies ran while one was open for 20% of the time, Pallas kernels for 0%

commit v1 on v0

--- a/solution.py
+++ b/solution.py
@@ -145,8 +145,14 @@
     weights = powers / jnp.sum(powers, axis=-1, keepdims=True)
     weights_low = weights.astype(BF)
     attended = bmm(weights_low, values, ((2,), (1,))).astype(BF)
-    merged = lax.all_to_all(
-        jnp.swapaxes(attended, 0, 1), "seq", split_axis=0, concat_axis=1, tiled=True
+    merged = jnp.concatenate(
+        lax.all_to_all(
+            jnp.stack(jnp.split(jnp.swapaxes(attended, 0, 1), lax.axis_size("seq"), axis=0)),
+            "seq",
+            0,
+            0,
+        ),
+        axis=1,
     ).reshape(rows, H * HD)
     inputs = tokens[0].astype(F32)
     residual = inputs + nn(merged, out_full)

time: 1470 us -> 1470 us (level)
  no operation moved by 1% of the time
where the time goes in v1:
time: 1470 us; the launch traced here: 1460 us
  waiting for transfers between devices  979 us (67%)
  matrix products  201 us (14%)
  local copies, waits for them, and re-layouts  134 us (9%)
  other arithmetic  88.9 us (6%)
  blocking collectives  33.3 us (2%)
  between operations  16 us (1%)
    reduce_scatter x4, waiting for transfers between devices, body(): lax.psum_scatter(joined, 'wt', scatter_dimension=0, tiled=False).astype(F32)  369 us
    all_gather x4, waiting for transfers between devices, body(): lax.all_gather(jnp.concatenate([w_gate_up[e], w_down[e]], axis=0), 'wt',...  249 us
    dot_general x34, matrix products, dot(): lax.dot_general(left, right, (dims, ((), ())), preferred_element_type=F32)  188 us
    all_gather x1, waiting for transfers between devices, body(): collected = lax.all_gather(scattered, 'seq', axis=0).astype(F32)  59.4 us
    psum x1, waiting for transfers between devices, body(): out_grad = lax.psum(out_grad, 'seq').astype(F32)  49.5 us
    all_gather x1, waiting for transfers between devices, body(): lax.all_gather(jnp.concatenate([w_here, small], axis=1), 'wt', axis=0, ti...  48.1 us
    reduce_scatter x1, waiting for transfers between devices, body(): lax.psum_scatter(out_part.astype(BF), 'seq', scatter_dimension=0, tiled=T...  40.3 us
    all_gather x1, waiting for transfers between devices, body(): tokens_all = lax.all_gather(tokens[0], 'seq', axis=0, tiled=True)  39.6 us
  transfers between devices with their start and end apart: 21, of which 20 were waited for; matrix products, arithmetic and copies ran while one was open for 20% of the time, Pallas kernels for 0%

profile of v1, /device:TPU:0, one launch (start us, length us, event | category | flops | bytes accessed | tf_op | source)
XLA Modules:
  0.0 1457.5 jit_solution(7589946342975081403)
XLA Ops:
  18.4 39.6 %all-gather.25.cloned.1.call-done = bf16[1,512,2048]{2,1,0:T(8,128)(2,1)} async-done(((bf16[1,128,2048]{2,1,0:T(8,128)(2,1)}), bf16[1,512,2048]{2,1,0:T(8,128)(2,1)}) %all-gather.25.cloned.1.call-update) | async-done | bytes 2097168 | tf_op jit(solution)/shard_map/all_gather | solution.py:94
  60.1 48.1 %all-gather.19.cloned.1.call-done = bf16[2048,1664]{0,1:T(8,128)(2,1)} async-done(((bf16[256,1664]{0,1:T(8,128)(2,1)}), bf16[2048,1664]{0,1:T(8,128)(2,1)}) %all-gather.19.cloned.1.call-update) | async-done | bytes 6815760 | tf_op jit(solution)/shard_map/all_gather | solution.py:110
  110.0 8.6 fusion.3
  133.4 19.5 %all_to_all.23 = bf16[4,128,4,128]{3,1,2,0:T(8,128)(2,1)S(1)} all-to-all(bf16[4,128,4,128]{3,1,2,0:T(8,128)(2,1)S(1)} %pad_maximum_fusion.25), channel_id=1, replica_groups=mesh['seq'=4,'wt'=8] {'seq'}, dimensions={0} | all-to-all | bytes 1048576 | tf_op jit(solution)/shard_map/all_to_all | solution.py:149
  153.2 11.2 all-gather.21.cloned.1.call-done
  164.4 4.9 multiply_reduce_fusion.7
  182.9 13.8 all-gather.1
  196.9 20.4 %all-gather.23.cloned.1.call-done = bf16[512,2048]{1,0:T(8,128)(2,1)} async-done(((bf16[128,2048]{1,0:T(8,128)(2,1)}), bf16[512,2048]{1,0:T(8,128)(2,1)}) %all-gather.23.cloned.1.call-update) | async-done | bytes 2097168 | tf_op jit(solution)/shard_map/all_gather | solution.py:161
  222.5 68.0 %all-gather.31.cloned.1.call-done = bf16[3072,2048]{1,0:T(8,128)(2,1)} async-done(((bf16[384,2048]{1,0:T(8,128)(2,1)}), bf16[3072,2048]{1,0:T(8,128)(2,1)}) %all-gather.31.cloned.1.call-update) | async-done | bytes 12582928 | tf_op jit(solution)/shard_map/all_gather | solution.py:114
  290.4 8.4 slice.299
  298.9 5.4 slice.302
  304.3 60.5 %all-gather.27.cloned.1.call-done = bf16[3072,2048]{1,0:T(8,128)(2,1)} async-done(((bf16[384,2048]{1,0:T(8,128)(2,1)}), bf16[3072,2048]{1,0:T(8,128)(2,1)}) %all-gather.27.cloned.1.call-update) | async-done | bytes 12582928 | tf_op jit(solution)/shard_map/all_gather | solution.py:114
  364.8 8.3 slice.291
  373.1 5.4 slice.294
  378.5 60.2 %all-gather.29.cloned.1.call-done = bf16[3072,2048]{1,0:T(8,128)(2,1)} async-done(((bf16[384,2048]{1,0:T(8,128)(2,1)}), bf16[3072,2048]{1,0:T(8,128)(2,1)}) %all-gather.29.cloned.1.call-update) | async-done | bytes 12582928 | tf_op jit(solution)/shard_map/all_gather | solution.py:114
  438.7 8.3 slice.295
  447.0 5.5 slice.298
  452.5 60.1 %all-gather.33.cloned.1.call-done = bf16[3072,2048]{1,0:T(8,128)(2,1)} async-done(((bf16[384,2048]{1,0:T(8,128)(2,1)}), bf16[3072,2048]{1,0:T(8,128)(2,1)}) %all-gather.33.cloned.1.call-update) | async-done | bytes 12582928 | tf_op jit(solution)/shard_map/all_gather | solution.py:114
  512.6 8.3 slice.303
  520.9 5.2 slice.306
  526.1 9.6 fusion.110
  535.7 6.2 fusion.106
  541.9 6.2 fusion.108
  548.2 6.5 fusion.112
  554.7 5.2 all-gather.35.cloned.1.call-done
  559.9 9.1 multiply_convert_fusion.4
  569.0 4.6 multiply_convert_fusion.8
  573.7 5.0 multiply_convert_fusion.6
  578.6 4.6 multiply_convert_fusion.2
  583.8 10.7 fusion.39
  594.5 9.7 fusion.41
  604.3 6.2 fusion.40
  611.6 12.3 add_convert_fusion
  626.9 5.0 fusion.111
  642.2 30.1 %reduce-scatter.12.cloned.1.call-done = bf16[128,2080]{1,0:T(8,128)(2,1)} async-done(((bf16[512,2080]{1,0:T(8,128)(2,1)}), bf16[128,2080]{1,0:T(8,128)(2,1)}) %reduce-scatter.12.cloned.1.call-update) | async-done | bytes 532496 | tf_op jit(solution)/shard_map/reduce_scatter | solution.py:213
  677.7 40.3 %reduce-scatter.10.cloned.1.call-done = bf16[128,2048]{1,0:T(8,128)(2,1)} async-done(((bf16[512,2048]{1,0:T(8,128)(2,1)}), bf16[128,2048]{1,0:T(8,128)(2,1)}) %reduce-scatter.10.cloned.1.call-update) | async-done | bytes 524304 | tf_op jit(solution)/shard_map/reduce_scatter | solution.py:221
  720.6 5.7 convolution_convert_fusion.5
  726.4 6.4 fusion.46
  737.5 14.1 all-to-all-done.1
  768.3 9.8 fusion.8
  778.4 5.6 convolution_convert_fusion
  784.1 7.9 fusion.2
  792.6 4.6 reduce-scatter.18.cloned.1.call-done
  797.5 6.9 convolution_convert_fusion.1
  806.9 9.1 pad_maximum_fusion.3
  817.3 4.1 convolution_convert_fusion.7
  821.5 5.0 convolution_convert_fusion.2
  826.5 9.2 pad_maximum_fusion.2
  836.8 4.2 convolution_convert_fusion.8
  841.1 5.0 convolution_convert_fusion.3
  846.1 9.1 pad_maximum_fusion.1
  860.6 5.0 convolution_convert_fusion.4
  865.6 9.0 pad_maximum_fusion
  875.9 35.2 %reduce-scatter.14.cloned.1.call-done = bf16[128,2048]{1,0:T(8,128)(2,1)} async-done(((bf16[512,2048]{1,0:T(8,128)(2,1)}), bf16[128,2048]{1,0:T(8,128)(2,1)}) %reduce-scatter.14.cloned.1.call-update) | async-done | bytes 524304 | tf_op jit(solution)/shard_map/reduce_scatter | solution.py:268
  914.9 49.5 %all-reduce.9.cloned.1.call-done = bf16[256,2048]{1,0:T(8,128)(2,1)} async-done(((bf16[256,2048]{1,0:T(8,128)(2,1)}), bf16[256,2048]{1,0:T(8,128)(2,1)}) %all-reduce.9.cloned.1.call-update) | async-done | bytes 1048592 | tf_op jit(solution)/shard_map/psum | solution.py:249
  967.2 92.2 %reduce-scatter.26.cloned.1.call-done = bf16[1,384,2048]{2,1,0:T(8,128)(2,1)} async-done(((bf16[8,384,2048]{2,1,0:T(8,128)(2,1)}), bf16[1,384,2048]{2,1,0:T(8,128)(2,1)}) %reduce-scatter.26.cloned.1.call-update) | async-done | bytes 1572880 | tf_op jit(solution)/shard_map/reduce_scatter | solution.py:202
  1061.2 93.8 %reduce-scatter.24.cloned.1.call-done = bf16[1,384,2048]{2,1,0:T(8,128)(2,1)} async-done(((bf16[8,384,2048]{2,1,0:T(8,128)(2,1)}), bf16[1,384,2048]{2,1,0:T(8,128)(2,1)}) %reduce-scatter.24.cloned.1.call-update) | async-done | bytes 1572880 | tf_op jit(solution)/shard_map/reduce_scatter | solution.py:202
  1159.1 91.7 %reduce-scatter.22.cloned.1.call-done = bf16[1,384,2048]{2,1,0:T(8,128)(2,1)} async-done(((bf16[8,384,2048]{2,1,0:T(8,128)(2,1)}), bf16[1,384,2048]{2,1,0:T(8,128)(2,1)}) %reduce-scatter.22.cloned.1.call-update) | async-done | bytes 1572880 | tf_op jit(solution)/shard_map/reduce_scatter | solution.py:202
  1254.8 91.8 %reduce-scatter.20.cloned.1.call-done = bf16[1,384,2048]{2,1,0:T(8,128)(2,1)} async-done(((bf16[8,384,2048]{2,1,0:T(8,128)(2,1)}), bf16[1,384,2048]{2,1,0:T(8,128)(2,1)}) %reduce-scatter.20.cloned.1.call-update) | async-done | bytes 1572880 | tf_op jit(solution)/shard_map/reduce_scatter | solution.py:202
  1356.3 59.4 %all-gather.37.cloned.1.call-done = bf16[1024,1664]{0,1:T(8,128)(2,1)} async-done(((bf16[256,1664]{0,1:T(8,128)(2,1)}), bf16[1024,1664]{0,1:T(8,128)(2,1)}) %all-gather.37.cloned.1.call-update) | async-done | bytes 3407888 | tf_op jit(solution)/shard_map/all_gather | solution.py:296
  1415.7 7.9 reshape.382
  1423.6 6.8 slice.314
  1433.4 8.7 copy.156
  1442.1 8.3 reshape.362
  (379 shorter events, 134.4 us)
Async XLA Ops:
  7.2 6.7 copy-start.69
  7.2 50.8 %all-gather.25.cloned.1.call-start = ((), (), s32[]{:S(2)}) async-start(), calls=%async_computation.24 | async-start | bytes 2621440 | tf_op jit(solution)/shard_map/all_gather | solution.py:94
  7.9 100.2 %all-gather.19.cloned.1.call-start = ((), (), s32[]{:S(2)}) async-start(), calls=%async_computation.11 | async-start | bytes 7667712 | tf_op jit(solution)/shard_map/all_gather | solution.py:110
  10.6 5.1 copy-start.63
  13.8 94.4 %copy-start.73 = (bf16[8,128]{1,0:T(8,128)(2,1)S(1)}, bf16[8,128]{1,0:T(8,128)(2,1)}, u32[]{:S(2)}) copy-start(bf16[8,128]{1,0:T(8,128)(2,1)} %constant.61.clone) | copy-start | bytes 6148
  14.9 149.4 %all-gather.21.cloned.1.call-start = ((), (), s32[]{:S(2)}) async-start(), calls=%async_computation.12 | async-start | bytes 9437184 | tf_op jit(solution)/shard_map/all_gather | solution.py:111
  15.7 201.6 %all-gather.23.cloned.1.call-start = ((), (), s32[]{:S(2)}) async-start(), calls=%async_computation.13 | async-start | bytes 2621440 | tf_op jit(solution)/shard_map/all_gather | solution.py:161
  18.4 106.8 %copy-start.28 = (f32[512,64]{1,0:T(8,128)}, f32[512,64]{1,0:T(8,128)S(1)}, u32[]{:S(2)}) copy-start(f32[512,64]{1,0:T(8,128)S(1)} %get-tuple-element.81) | copy-start | bytes 393220
  60.1 49.4 %copy-start.74 = (f32[512]{0:T(512)}, f32[512]{0:T(512)S(1)}, u32[]{:S(2)}) copy-start(f32[512]{0:T(512)S(1)} %add_rsqrt_fusion.2) | copy-start | bytes 6148
  109.5 59.8 %copy-start.53 = (f32[1,2048]{1,0:T(1,128)}, f32[1,2048]{1,0:T(1,128)S(1)}, u32[]{:S(2)}) copy-start(f32[1,2048]{1,0:T(1,128)S(1)} %get-tuple-element.77) | copy-start | bytes 24580
  133.3 31.1 %copy-start.6 = (bf16[1,128,2048]{2,1,0:T(8,128)(2,1)S(1)}, bf16[1,128,2048]{2,1,0:T(8,128)(2,1)}, u32[]{:S(2)}) copy-start(bf16[1,128,2048]{2,1,0:T(8,128)(2,1)} %param.14) | copy-start | bytes 1572868
  153.2 16.1 %copy-start.8 = (bf16[128,4,4,128]{0,3,2,1:T(8,128)(2,1)}, bf16[128,4,4,128]{0,3,2,1:T(8,128)(2,1)S(1)}, u32[]{:S(2)}) copy-start(bf16[128,4,4,128]{0,3,2,1:T(8,128)(2,1)S(1)} %copy.134) | copy-start | bytes 1572868
  164.4 6.9 copy-start.34
  169.3 5.2 copy-start.70
  171.2 119.2 %all-gather.31.cloned.1.call-start = ((), (), s32[]{:S(2)}) async-start(), calls=%async_computation.27 | async-start | bytes 14155776 | tf_op jit(solution)/shard_map/all_gather | solution.py:114
  175.8 189.0 %all-gather.27.cloned.1.call-start = ((), (), s32[]{:S(2)}) async-start(), calls=%async_computation.25 | async-start | bytes 14155776 | tf_op jit(solution)/shard_map/all_gather | solution.py:114
  178.2 260.5 %all-gather.29.cloned.1.call-start = ((), (), s32[]{:S(2)}) async-start(), calls=%async_computation.26 | async-start | bytes 14155776 | tf_op jit(solution)/shard_map/all_gather | solution.py:114
  180.8 331.8 %all-gather.33.cloned.1.call-start = ((), (), s32[]{:S(2)}) async-start(), calls=%async_computation.28 | async-start | bytes 14155776 | tf_op jit(solution)/shard_map/all_gather | solution.py:114
  182.1 377.8 %all-gather.35.cloned.1.call-start = ((), (), s32[]{:S(2)}) async-start(), calls=%async_computation.29 | async-start | bytes 2621440 | tf_op jit(solution)/shard_map/all_gather | solution.py:112
  182.9 489.4 %reduce-scatter.12.cloned.1.call-start = ((), (), s32[]{:S(2)}) async-start(), calls=%async_computation.15 | async-start | bytes 2785280 | tf_op jit(solution)/shard_map/reduce_scatter | solution.py:213
  196.9 102.0 %copy-start.49 = (pred[512,16]{1,0:T(8,128)(4,1)}, pred[512,16]{1,0:T(8,128)(4,1)S(1)}, u32[]{:S(2)}) copy-start(pred[512,16]{1,0:T(8,128)(4,1)S(1)} %copy.136) | copy-start | bytes 24580
  220.2 78.6 %copy-start.64 = (f32[512]{0:T(512)}, f32[512]{0:T(512)S(1)}, u32[]{:S(2)}) copy-start(f32[512]{0:T(512)S(1)} %get-tuple-element.25) | copy-start | bytes 6148
  520.9 5.2 copy-start.30
  520.9 14.8 %slice-start = ((s8[8388608]{0:T(1024)(128)(4,1)}), s8[4194304]{0:T(1024)(128)(4,1)S(1)}, s32[]{:S(2)}) async-start(s8[8388608]{0:T(1024)(128)(4,1)} %bitcast.305), calls=%async_computation.31 | async-start | bytes 8388608
  526.1 9.6 slice-start.1
  526.1 15.8 %slice-start.4 = ((s8[8388608]{0:T(1024)(128)(4,1)}), s8[4194304]{0:T(1024)(128)(4,1)S(1)}, s32[]{:S(2)}) async-start(s8[8388608]{0:T(1024)(128)(4,1)} %bitcast.312), calls=%async_computation.35 | async-start | bytes 8388608
  535.7 6.2 slice-start.5
  535.7 12.5 slice-start.2
  541.9 6.2 slice-start.3
  559.9 9.1 copy-start.20
  559.9 9.1 copy-start.76
  559.9 9.1 copy-start.87
  573.6 20.9 %copy-start.88 = (bf16[512,1024]{1,0:T(8,128)(2,1)}, bf16[512,1024]{1,0:T(8,128)(2,1)S(1)}, u32[]{:S(2)}) copy-start(bf16[512,1024]{1,0:T(8,128)(2,1)S(1)} %get-tuple-element.31) | copy-start | bytes 3145732
  583.2 53.8 %copy-start.78 = (bf16[512,1024]{1,0:T(8,128)(2,1)}, bf16[512,1024]{1,0:T(8,128)(2,1)S(1)}, u32[]{:S(2)}) copy-start(bf16[512,1024]{1,0:T(8,128)(2,1)S(1)} %get-tuple-element.39) | copy-start | bytes 3145732
  583.8 10.7 copy-start.90
  583.8 20.5 %slice-start.6 = ((s8[8388608]{0:T(1024)(128)(4,1)}), s8[4194304]{0:T(1024)(128)(4,1)S(1)}, s32[]{:S(2)}) async-start(s8[8388608]{0:T(1024)(128)(4,1)} %bitcast.315), calls=%async_computation.37 | async-start | bytes 8388608
  594.5 9.7 slice-start.7
  594.5 9.7 copy-start.92
  594.5 9.7 copy-start.94
  626.8 91.3 %reduce-scatter.10.cloned.1.call-start = ((), (), s32[]{:S(2)}) async-start(), calls=%async_computation.14 | async-start | bytes 2621440 | tf_op jit(solution)/shard_map/reduce_scatter | solution.py:221
  626.8 5.0 copy-start.21
  626.8 5.0 copy-start.80
  637.1 37.4 %copy-start.46 = (f32[512,16]{1,0:T(8,128)S(1)}, f32[512,16]{1,0:T(8,128)}, u32[]{:S(2)}) copy-start(f32[512,16]{1,0:T(8,128)} %copy-done.45) | copy-start | bytes 98308
  640.9 34.6 %copy-start.5 = (f32[128,2048]{1,0:T(8,128)S(1)}, f32[128,2048]{1,0:T(8,128)}, u32[]{:S(2)}) copy-start(f32[128,2048]{1,0:T(8,128)} %copy-done.4) | copy-start | bytes 3145732
  640.9 34.6 %copy-start.54 = (f32[1,2048]{1,0:T(1,128)S(1)}, f32[1,2048]{1,0:T(1,128)}, u32[]{:S(2)}) copy-start(f32[1,2048]{1,0:T(1,128)} %copy-done.53) | copy-start | bytes 24580
  640.9 34.6 %copy-start.71 = (f32[128]{0:T(128)S(1)}, f32[128]{0:T(128)}, u32[]{:S(2)}) copy-start(f32[128]{0:T(128)} %copy-done.70) | copy-start | bytes 1540
  640.9 77.1 %copy-start.35 = (bf16[1,128,2048]{2,1,0:T(8,128)(2,1)S(1)}, bf16[1,128,2048]{2,1,0:T(8,128)(2,1)}, u32[]{:S(2)}) copy-start(bf16[1,128,2048]{2,1,0:T(8,128)(2,1)} %param.15) | copy-start | bytes 1572868
  640.9 156.3 %reduce-scatter.18.cloned.1.call-start = ((), (), s32[]{:S(2)}) async-start(), calls=%async_computation.18 | async-start | bytes 9437184 | tf_op jit(solution)/shard_map/reduce_scatter | solution.py:246
  674.4 46.2 %copy-start.9 = (bf16[128,4,4,128]{0,3,2,1:T(8,128)(2,1)S(1)}, bf16[128,4,4,128]{0,3,2,1:T(8,128)(2,1)}, u32[]{:S(2)}) copy-start(bf16[128,4,4,128]{0,3,2,1:T(8,128)(2,1)} %copy-done.8) | copy-start | bytes 1572868
  726.3 10.9 copy-start.17
  726.3 25.2 %copy-start.51 = (bf16[512,1,4,128]{3,2,1,0:T(4,128)(2,1)S(1)}, bf16[512,1,4,128]{3,2,1,0:T(4,128)(2,1)}, u32[]{:S(2)}) copy-start(bf16[512,1,4,128]{3,2,1,0:T(4,128)(2,1)} %slice.288) | copy-start | bytes 1572868
  726.4 25.2 %copy-start.62 = (f32[4,512]{1,0:T(4,128)S(1)}, f32[4,512]{1,0:T(4,128)}, u32[]{:S(2)}) copy-start(f32[4,512]{1,0:T(4,128)} %copy-done.61) | copy-start | bytes 24580
  733.7 17.9 %all-to-all-start.1 = ((bf16[128,16,128]{2,0,1:T(8,128)(2,1)}), bf16[128,16,128]{2,0,1:T(8,128)(2,1)S(1)}, u32[]{:S(2)}, u32[]{:S(2)}) async-start(bf16[128,16,128]{2,0,1:T(8,128)(2,1)} %bitcast.281), calls=%async_computation.3 | async-start | bytes 1048576 | tf_op jit(solution)/shard_map/all_to_all | solution.py:244
  737.2 137.6 %reduce-scatter.16.cloned.1.call-start = ((), (), s32[]{:S(2)}) async-start(), calls=%async_computation.17 | async-start | bytes 7667712 | tf_op jit(solution)/shard_map/reduce_scatter | solution.py:290
  768.3 10.1 copy-start.60
  792.0 119.2 %reduce-scatter.14.cloned.1.call-start = ((), (), s32[]{:S(2)}) async-start(), calls=%async_computation.16 | async-start | bytes 2621440 | tf_op jit(solution)/shard_map/reduce_scatter | solution.py:268
  792.5 171.9 %all-reduce.9.cloned.1.call-start = ((), (), s32[]{:S(2)}) async-start(), calls=%async_computation.19 | async-start | bytes 2097152 | tf_op jit(solution)/shard_map/psum | solution.py:249
  797.3 7.2 copy-start.79
  797.3 262.1 %reduce-scatter.26.cloned.1.call-start = ((), (), s32[]{:S(2)}) async-start(), calls=%async_computation.23 | async-start | bytes 14155776 | tf_op jit(solution)/shard_map/reduce_scatter | solution.py:202
  797.5 6.9 copy-start.77
  816.0 339.0 %reduce-scatter.24.cloned.1.call-start = ((), (), s32[]{:S(2)}) async-start(), calls=%async_computation.22 | async-start | bytes 14155776 | tf_op jit(solution)/shard_map/reduce_scatter | solution.py:202
  835.6 415.1 %reduce-scatter.22.cloned.1.call-start = ((), (), s32[]{:S(2)}) async-start(), calls=%async_computation.21 | async-start | bytes 14155776 | tf_op jit(solution)/shard_map/reduce_scatter | solution.py:202
  855.3 491.3 %reduce-scatter.20.cloned.1.call-start = ((), (), s32[]{:S(2)}) async-start(), calls=%async_computation.20 | async-start | bytes 14155776 | tf_op jit(solution)/shard_map/reduce_scatter | solution.py:202
  874.7 541.0 %all-gather.37.cloned.1.call-start = ((), (), s32[]{:S(2)}) async-start(), calls=%async_computation.30 | async-start | bytes 4259840 | tf_op jit(solution)/shard_map/all_gather | solution.py:296
  (63 other events, 161.4 us)
Sparse Core Ops, SparseCore 0:
  9.6 48.3 all-gather.24
  60.4 47.6 all-gather.18
  110.1 54.2 all-gather.20
  171.3 45.9 all-gather.22
  219.6 70.7 all-gather.30
  292.8 71.9 all-gather.26
  366.7 71.9 all-gather.28
  440.6 71.9 all-gather.32
  514.2 45.6 all-gather.34
  626.9 45.2 reduce-scatter.11
  675.1 42.8 reduce-scatter.9
  726.5 70.7 reduce-scatter.17
  800.7 64.0 reduce-scatter.15
  867.5 43.6 reduce-scatter.13
  913.3 51.0 all-reduce.8
  967.8 91.5 reduce-scatter.25
  1062.7 92.2 reduce-scatter.23
  1158.4 92.2 reduce-scatter.21
  1254.2 92.2 reduce-scatter.19
  1348.0 67.6 all-gather.36
